TPU v7x, 32 devices: a whole 2x2x4 slice. The times are simulated.
32 devices in a mesh: dp: 4 (over x, core), fsdp: 4 (over z), tp: 2 (over y).
Axes of the slice: x: 2, y: 2, z: 4, core: 2. Of those that a mesh axis runs over, the one named last changes fastest.
Arguments:
- hidden: bfloat16 [8192, 7168], P(('dp', 'fsdp')), may hold values from -6 to 6
- cotangent: bfloat16 [8192, 576], P(('dp', 'fsdp'), 'tp'), may hold values from -6 to 6
- rewards: int32 [64], P(('dp', 'fsdp')), may hold values from 0 to 8
- groups: int32 [64], P(('dp', 'fsdp')), may hold values from 0 to 3, as said below
- lengths: int32 [64], P(('dp', 'fsdp')), may hold values from 1 to 128
- master: float32 [4, 1792, 576], P('fsdp', 'dp', 'tp'), may hold values from -6 to 6
Outputs:
- grad_owned: float32 [4, 1792, 576], P('fsdp', 'dp', 'tp')
- rollout: bfloat16 [4, 1792, 576], P('fsdp')
Inputs may be any that keep to these rules, and one draw needn't show every extreme that they name: `groups`: each prompt number names exactly 16 samples.
All inputs are finite; a program needn't handle non-finite values.
Results may differ from a plain program's by a relative error of at most 0.0033.
Values may be sent and summed in bfloat16 or wider, within the bound.
A program may use at most 64 MiB of HBM per device.

v0:
```python
import jax
import jax.numpy as jnp
from jax import lax
from jax.sharding import PartitionSpec as P

D = 7168
GROUP = 16


def exact_dot(left, right):
    return jnp.dot(left, right, precision=lax.Precision.HIGHEST)


def shards(hidden, cotangent, rewards, groups, lengths, master):
    fsdp_size = lax.axis_size("fsdp")
    dp_size = lax.axis_size("dp")
    samp_local = rewards.shape[0]
    group_count = samp_local * dp_size * fsdp_size // GROUP
    labels = jnp.arange(group_count, dtype=jnp.int32)
    reward_f = rewards.astype(jnp.float32)
    local_onehot = (groups[:, None] == labels[None, :]).astype(jnp.float32)
    totals, squares = lax.psum(
        (exact_dot(reward_f, local_onehot), exact_dot(reward_f * reward_f, local_onehot)),
        ("dp", "fsdp"),
    )
    group_mean = totals / GROUP
    group_square = squares / GROUP
    sample_mean = exact_dot(local_onehot, group_mean)
    sample_square = exact_dot(local_onehot, group_square)
    advantage = (reward_f - sample_mean) / jnp.sqrt(sample_square - sample_mean * sample_mean + 1.0)
    seq_len = hidden.shape[0] // samp_local
    positions = jnp.arange(seq_len, dtype=jnp.int32)
    live = (positions[None, :] < lengths[:, None]).astype(jnp.float32)
    scale = (advantage[:, None] * live / lengths[:, None].astype(jnp.float32)).reshape(
        hidden.shape[0]
    )
    weighted = (cotangent.astype(jnp.float32) * scale[:, None]).astype(jnp.bfloat16)
    cols_local = cotangent.shape[1]
    block_rows = D // fsdp_size
    product = jnp.einsum("td,tc->dc", hidden, weighted, preferred_element_type=jnp.float32)
    reduced = lax.psum_scatter(
        product.reshape(1 * lax.axis_size("fsdp"), block_rows, cols_local),
        "fsdp",
        scatter_dimension=0,
        tiled=True,
    )
    owned = lax.psum_scatter(reduced, "dp", scatter_dimension=1, tiled=True)
    updated = (master - 0.1 * owned).astype(jnp.bfloat16)
    full_rows = lax.all_gather(updated, "tp", axis=2, tiled=True)
    rollout = lax.all_gather(full_rows, "dp", axis=1, tiled=True)
    return (owned, rollout)


def solution(mesh):
    placed = (
        P(("dp", "fsdp"), None),
        P(("dp", "fsdp"), "tp"),
        P(("dp", "fsdp")),
        P(("dp", "fsdp")),
        P(("dp", "fsdp")),
        P("fsdp", "dp", "tp"),
    )
    return jax.shard_map(
        shards,
        mesh=mesh,
        in_specs=placed,
        out_specs=(P("fsdp", "dp", "tp"), P("fsdp", None, None)),
        check_vma=False,
    )
```

profile of v0, /device:TPU:0, one launch (start us, length us, event | category | flops | bytes accessed | tf_op | source)
XLA Modules:
  0.0 288.7 jit_solution(1073819493120630368)
XLA Ops:
  7.2 0.0 reduce-scatter.5.cloned.1.call-start
  7.2 0.9 convolution_bitcast_fusion.1
  8.1 0.9 convolution_bitcast_fusion.3
  8.9 0.7 convert_element_type.20
  9.6 35.1 %all-reduce = (f32[4]{0:T(128)S(1)}, f32[4]{0:T(128)S(1)}) all-reduce(f32[4]{0:T(128)S(1)} %convolution_bitcast_fusion.3, f32[4]{0:T(128)S(1)} %convolution_bitcast_fusion.1), channel_id=1, replica_groups=mesh['dp'=4,'fsdp'=4,'tp'=2] {'dp','fsdp'}, use_global_device_ids=true, to_apply=%region_0.0 | all-reduce | flops 8 | bytes 64 | tf_op jit(solution)/shard_map/psum | solution.py:22
  44.7 0.8 convolution_bitcast_fusion.2
  45.6 0.9 fusion.3
  46.4 0.7 divide_bitcast_fusion
  47.2 5.5 %fusion.4 = f32[288,7168]{1,0:T(8,128)S(1)} fusion(bf16[512,7168]{1,0:T(8,128)(2,1)} %param.6, bf16[512,288]{0,1:T(8,128)(2,1)} %param.7, f32[512]{0:T(512)S(1)} %divide_bitcast_fusion), kind=kOutput, calls=%fused_computation.13 | convolution fusion | flops 2114371584 | bytes 15894528 | tf_op jit(solution)/shard_map/td,tc->dc/dot_general | solution.py:40
  52.7 3.8 %copy.18 = f32[36,4,8,1792]{3,2,0,1:T(8,128)} copy(f32[36,4,8,1792]{3,2,1,0:T(8,128)S(1)} %bitcast.43) | data formatting | bytes 16515072 | tf_op jit(solution)/shard_map/reshape | solution.py:42
  56.5 0.0 reduce-scatter.5.cloned.1.call-update
  56.5 0.0 copy-start.1
  56.6 0.0 reduce-scatter.7.cloned.1.call-start
  56.6 139.9 %reduce-scatter.5.cloned.1.call-done = f32[1,1792,288]{1,2,0:T(8,128)} async-done(((f32[4,1792,288]{1,2,0:T(8,128)}), f32[1,1792,288]{1,2,0:T(8,128)}) %reduce-scatter.5.cloned.1.call-update) | async-done | bytes 2064400 | tf_op jit(solution)/shard_map/reduce_scatter | solution.py:41
  196.5 6.9 %copy.12 = f32[1,1792,288]{2,0,1:T(1,128)S(1)} copy(f32[1,1792,288]{1,2,0:T(8,128)} %reduce-scatter.5.cloned.1.call-done) | data formatting | bytes 4128768
  203.4 1.7 copy.19
  205.1 0.0 reduce-scatter.7.cloned.1.call-update
  205.1 0.0 all-gather.2.cloned.1.call-start
  205.2 36.0 %reduce-scatter.7.cloned.1.call-done = f32[448,288]{1,0:T(8,128)} async-done(((f32[1792,288]{1,0:T(8,128)}), f32[448,288]{1,0:T(8,128)}) %reduce-scatter.7.cloned.1.call-update) | async-done | bytes 516112
  241.2 1.6 reshape_bitcast_fusion
  242.8 1.0 copy.13
  243.8 0.0 copy-done.1
  243.8 0.0 copy-start
  243.8 0.1 subtract_convert_fusion
  243.9 9.2 %all_gather.6 = bf16[1,448,576]{1,2,0:T(8,128)(2,1)S(1)} all-gather(bf16[1,448,288]{1,2,0:T(8,128)(2,1)S(1)} %subtract_convert_fusion), channel_id=1, replica_groups=mesh['dp'=4,'fsdp'=4,'tp'=2] {'tp'}, dimensions={2}, use_global_device_ids=true | all-gather | bytes 774144 | tf_op jit(solution)/shard_map/all_gather | solution.py:49
  253.2 1.1 copy.10
  254.2 0.0 all-gather.2.cloned.1.call-update
  254.3 23.8 %all-gather.2.cloned.1.call-done = bf16[1,1792,576]{2,1,0:T(8,128)(2,1)} async-done(((bf16[1,448,576]{2,1,0:T(8,128)(2,1)}), bf16[1,1792,576]{2,1,0:T(8,128)(2,1)}) %all-gather.2.cloned.1.call-update) | async-done | bytes 2064400 | tf_op jit(solution)/shard_map/all_gather | solution.py:50
  278.1 4.1 %copy.11 = bf16[1,1792,576]{1,2,0:T(8,128)(2,1)} copy(bf16[1,1792,576]{2,1,0:T(8,128)(2,1)} %all-gather.2.cloned.1.call-done) | data formatting | bytes 4128768
  282.2 0.0 copy-done
Async XLA Ops:
  7.2 189.3 %reduce-scatter.5.cloned.1.call-start = ((), (), s32[]{:S(2)}) async-start(), calls=%async_computation.2 | async-start | bytes 10321920 | tf_op jit(solution)/shard_map/reduce_scatter | solution.py:41
  56.5 187.2 %copy-start.1 = (f32[1,448,288]{1,2,0:T(8,128)S(1)}, f32[1,448,288]{1,2,0:T(8,128)}, u32[]{:S(2)}) copy-start(f32[1,448,288]{1,2,0:T(8,128)} %param.11) | copy-start | bytes 1548292
  56.6 184.6 %reduce-scatter.7.cloned.1.call-start = ((), (), s32[]{:S(2)}) async-start(), calls=%async_computation.4 | async-start | bytes 3440640
  205.1 73.0 %all-gather.2.cloned.1.call-start = ((), (), s32[]{:S(2)}) async-start(), calls=%async_computation.3 | async-start | bytes 2867200 | tf_op jit(solution)/shard_map/all_gather | solution.py:50
  243.8 38.4 %copy-start = (f32[1,448,288]{1,2,0:T(8,128)}, f32[1,448,288]{1,2,0:T(8,128)S(1)}, u32[]{:S(2)}) copy-start(f32[1,448,288]{1,2,0:T(8,128)S(1)} %copy.13) | copy-start | bytes 1548292
Sparse Core Ops, SparseCore 0:
  56.7 139.7 reduce-scatter.4
  205.2 35.8 reduce-scatter.6
  254.4 23.6 all-gather.1
where the time goes:
time: 289 us
  waiting for transfers between devices  200 us (69%)
  blocking collectives  44.4 us (15%)
  local copies, waits for them, and re-layouts  20.2 us (7%)
  between operations  13.8 us (5%)
  matrix products  8.94 us (3%)
    reduce_scatter x1, waiting for transfers between devices, shards(): lax.psum_scatter(product.reshape(1 * lax.axis_size('fsdp'), block_rows, c...  140 us
    unnamed x4, waiting for transfers between devices  36.1 us
    psum x1, blocking collectives, shards(): lax.psum((exact_dot(reward_f, local_onehot), exact_dot(reward_f * reward_...  35.1 us
    all_gather x1, waiting for transfers between devices, shards(): rollout = lax.all_gather(full_rows, 'dp', axis=1, tiled=True)  23.8 us
    unnamed x9, local copies, waits for them, and re-layouts  15.3 us
    all_gather x1, blocking collectives, shards(): full_rows = lax.all_gather(updated, 'tp', axis=2, tiled=True)  9.24 us
  transfers between devices with their start and end apart: 3, of which 3 were waited for; matrix products, arithmetic and copies ran while one was open for 0% of the time, Pallas kernels for 0%

commit v1 on v0

--- a/solution.py
+++ b/solution.py
@@ -47,7 +47,7 @@
     owned = lax.psum_scatter(reduced, "dp", scatter_dimension=1, tiled=True)
     updated = (master - 0.1 * owned).astype(jnp.bfloat16)
     full_rows = lax.all_gather(updated, "tp", axis=2, tiled=True)
-    rollout = lax.all_gather(full_rows, "dp", axis=1, tiled=True)
+    rollout = jnp.concatenate(lax.all_gather(full_rows, "dp"), axis=1)
     return (owned, rollout)
 
 

time: 289 us -> 289 us (level)
  no operation moved by 1% of the time
where the time goes in v1:
time: 289 us
  waiting for transfers between devices  200 us (69%)
  blocking collectives  44.4 us (15%)
  local copies, waits for them, and re-layouts  20.2 us (7%)
  between operations  13.8 us (5%)
  matrix products  8.94 us (3%)
    reduce_scatter x1, waiting for transfers between devices, shards(): lax.psum_scatter(product.reshape(1 * lax.axis_size('fsdp'), block_rows, c...  140 us
    unnamed x4, waiting for transfers between devices  36.1 us
    psum x1, blocking collectives, shards(): lax.psum((exact_dot(reward_f, local_onehot), exact_dot(reward_f * reward_...  35.1 us
    all_gather x1, waiting for transfers between devices, shards(): rollout = jnp.concatenate(lax.all_gather(full_rows, 'dp'), axis=1)  23.8 us
    unnamed x9, local copies, waits for them, and re-layouts  15.3 us
    all_gather x1, blocking collectives, shards(): full_rows = lax.all_gather(updated, 'tp', axis=2, tiled=True)  9.24 us
  transfers between devices with their start and end apart: 3, of which 3 were waited for; matrix products, arithmetic and copies ran while one was open for 0% of the time, Pallas kernels for 0%

profile of v1, /device:TPU:0, one launch (start us, length us, event | category | flops | bytes accessed | tf_op | source)
XLA Modules:
  0.0 288.7 jit_solution(1073819493120630368)
XLA Ops:
  7.2 0.0 reduce-scatter.5.cloned.1.call-start
  7.2 0.9 convolution_bitcast_fusion.1
  8.1 0.9 convolution_bitcast_fusion.3
  8.9 0.7 convert_element_type.20
  9.6 35.1 %all-reduce = (f32[4]{0:T(128)S(1)}, f32[4]{0:T(128)S(1)}) all-reduce(f32[4]{0:T(128)S(1)} %convolution_bitcast_fusion.3, f32[4]{0:T(128)S(1)} %convolution_bitcast_fusion.1), channel_id=1, replica_groups=mesh['dp'=4,'fsdp'=4,'tp'=2] {'dp','fsdp'}, use_global_device_ids=true, to_apply=%region_0.0 | all-reduce | flops 8 | bytes 64 | tf_op jit(solution)/shard_map/psum | solution.py:22
  44.7 0.8 convolution_bitcast_fusion.2
  45.6 0.9 fusion.3
  46.4 0.7 divide_bitcast_fusion
  47.2 5.5 %fusion.4 = f32[288,7168]{1,0:T(8,128)S(1)} fusion(bf16[512,7168]{1,0:T(8,128)(2,1)} %param.6, bf16[512,288]{0,1:T(8,128)(2,1)} %param.7, f32[512]{0:T(512)S(1)} %divide_bitcast_fusion), kind=kOutput, calls=%fused_computation.13 | convolution fusion | flops 2114371584 | bytes 15894528 | tf_op jit(solution)/shard_map/td,tc->dc/dot_general | solution.py:40
  52.7 3.8 %copy.22 = f32[36,4,8,1792]{3,2,0,1:T(8,128)} copy(f32[36,4,8,1792]{3,2,1,0:T(8,128)S(1)} %bitcast.44) | data formatting | bytes 16515072 | tf_op jit(solution)/shard_map/reshape | solution.py:42
  56.5 0.0 reduce-scatter.5.cloned.1.call-update
  56.5 0.0 copy-start.1
  56.6 0.0 reduce-scatter.7.cloned.1.call-start
  56.6 139.9 %reduce-scatter.5.cloned.1.call-done = f32[1,1792,288]{1,2,0:T(8,128)} async-done(((f32[4,1792,288]{1,2,0:T(8,128)}), f32[1,1792,288]{1,2,0:T(8,128)}) %reduce-scatter.5.cloned.1.call-update) | async-done | bytes 2064400 | tf_op jit(solution)/shard_map/reduce_scatter | solution.py:41
  196.5 6.9 %copy.16 = f32[1,1792,288]{2,0,1:T(1,128)S(1)} copy(f32[1,1792,288]{1,2,0:T(8,128)} %reduce-scatter.5.cloned.1.call-done) | data formatting | bytes 4128768
  203.4 1.7 copy.23
  205.1 0.0 reduce-scatter.7.cloned.1.call-update
  205.1 0.0 all-gather.3.cloned.1.call-start
  205.2 36.0 %reduce-scatter.7.cloned.1.call-done = f32[448,288]{1,0:T(8,128)} async-done(((f32[1792,288]{1,0:T(8,128)}), f32[448,288]{1,0:T(8,128)}) %reduce-scatter.7.cloned.1.call-update) | async-done | bytes 516112
  241.2 1.6 reshape_bitcast_fusion
  242.8 1.0 copy.17
  243.8 0.0 copy-done.1
  243.8 0.0 copy-start
  243.8 0.1 subtract_convert_fusion
  243.9 9.2 %all_gather.9 = bf16[1,448,576]{1,2,0:T(8,128)(2,1)S(1)} all-gather(bf16[1,448,288]{1,2,0:T(8,128)(2,1)S(1)} %subtract_convert_fusion), channel_id=1, replica_groups=mesh['dp'=4,'fsdp'=4,'tp'=2] {'tp'}, dimensions={2}, use_global_device_ids=true | all-gather | bytes 774144 | tf_op jit(solution)/shard_map/all_gather | solution.py:49
  253.2 1.1 copy.14
  254.2 0.0 all-gather.3.cloned.1.call-update
  254.3 23.8 %all-gather.3.cloned.1.call-done = bf16[4,448,576]{2,1,0:T(8,128)(2,1)} async-done(((bf16[1,448,576]{2,1,0:T(8,128)(2,1)}), bf16[4,448,576]{2,1,0:T(8,128)(2,1)}) %all-gather.3.cloned.1.call-update) | async-done | bytes 2064400 | tf_op jit(solution)/shard_map/all_gather | solution.py:50
  278.1 4.1 %copy.15 = bf16[1,1792,576]{1,2,0:T(8,128)(2,1)} copy(bf16[1,1792,576]{2,1,0:T(8,128)(2,1)} %bitcast.48) | data formatting | bytes 4128768
  282.2 0.0 copy-done
Async XLA Ops:
  7.2 189.3 %reduce-scatter.5.cloned.1.call-start = ((), (), s32[]{:S(2)}) async-start(), calls=%async_computation.2 | async-start | bytes 10321920 | tf_op jit(solution)/shard_map/reduce_scatter | solution.py:41
  56.5 187.2 %copy-start.1 = (f32[1,448,288]{1,2,0:T(8,128)S(1)}, f32[1,448,288]{1,2,0:T(8,128)}, u32[]{:S(2)}) copy-start(f32[1,448,288]{1,2,0:T(8,128)} %param.11) | copy-start | bytes 1548292
  56.6 184.6 %reduce-scatter.7.cloned.1.call-start = ((), (), s32[]{:S(2)}) async-start(), calls=%async_computation.4 | async-start | bytes 3440640
  205.1 73.0 %all-gather.3.cloned.1.call-start = ((), (), s32[]{:S(2)}) async-start(), calls=%async_computation.3 | async-start | bytes 2867200 | tf_op jit(solution)/shard_map/all_gather | solution.py:50
  243.8 38.4 %copy-start = (f32[1,448,288]{1,2,0:T(8,128)}, f32[1,448,288]{1,2,0:T(8,128)S(1)}, u32[]{:S(2)}) copy-start(f32[1,448,288]{1,2,0:T(8,128)S(1)} %copy.17) | copy-start | bytes 1548292
Sparse Core Ops, SparseCore 0:
  56.7 139.7 reduce-scatter.4
  205.2 35.8 reduce-scatter.6
  254.4 23.6 all-gather.2

commit v2 on v0

--- a/solution.py
+++ b/solution.py
@@ -20,8 +20,11 @@
     reward_f = rewards.astype(jnp.float32)
     local_onehot = (groups[:, None] == labels[None, :]).astype(jnp.float32)
     totals, squares = lax.psum(
-        (exact_dot(reward_f, local_onehot), exact_dot(reward_f * reward_f, local_onehot)),
-        ("dp", "fsdp"),
+        lax.psum(
+            (exact_dot(reward_f, local_onehot), exact_dot(reward_f * reward_f, local_onehot)),
+            "fsdp",
+        ),
+        "dp",
     )
     group_mean = totals / GROUP
     group_square = squares / GROUP

time: 289 us -> 274 us (0.948)
  blocking collectives: 44.4 us -> 28.3 us
    psum x1, blocking collectives: 35.1 us -> 13.5 us  [shards(): lax.psum((exact_dot(reward_f, local_onehot), exact_dot(reward_f * reward_...]
    psum x0 -> x1, blocking collectives: none -> 5.65 us  [shards(): lax.psum(lax.psum((exact_dot(reward_f, local_onehot), exact_dot(reward_f...]
where the time goes in v2:
time: 274 us
  waiting for transfers between devices  201 us (73%)
  blocking collectives  28.3 us (10%)
  local copies, waits for them, and re-layouts  20.2 us (7%)
  between operations  13.8 us (5%)
  matrix products  8.93 us (3%)
    reduce_scatter x1, waiting for transfers between devices, shards(): lax.psum_scatter(product.reshape(1 * lax.axis_size('fsdp'), block_rows, c...  141 us
    unnamed x4, waiting for transfers between devices  36.1 us
    all_gather x1, waiting for transfers between devices, shards(): rollout = lax.all_gather(full_rows, 'dp', axis=1, tiled=True)  23.8 us
    unnamed x9, local copies, waits for them, and re-layouts  15.3 us
    psum x1, blocking collectives, shards(): lax.psum((exact_dot(reward_f, local_onehot), exact_dot(reward_f * reward_...  13.5 us
    all_gather x1, blocking collectives, shards(): full_rows = lax.all_gather(updated, 'tp', axis=2, tiled=True)  9.24 us
    psum x1, blocking collectives, shards(): lax.psum(lax.psum((exact_dot(reward_f, local_onehot), exact_dot(reward_f...  5.65 us
    dot_general x1, matrix products, shards(): jnp.einsum('td,tc->dc', hidden, weighted, preferred_element_type=jnp.floa...  5.5 us
  transfers between devices with their start and end apart: 3, of which 3 were waited for; matrix products, arithmetic and copies ran while one was open for 0% of the time, Pallas kernels for 0%

profile of v2, /device:TPU:0, one launch (start us, length us, event | category | flops | bytes accessed | tf_op | source)
XLA Modules:
  0.0 273.9 jit_solution(14867204249357697413)
XLA Ops:
  7.2 0.0 reduce-scatter.5.cloned.1.call-start
  7.2 0.9 convolution_bitcast_fusion.1
  8.1 0.9 convolution_bitcast_fusion.3
  8.9 0.7 convert_element_type.20
  9.6 13.5 %all-reduce = (f32[4]{0:T(128)S(1)}, f32[4]{0:T(128)S(1)}) all-reduce(f32[4]{0:T(128)S(1)} %convolution_bitcast_fusion.3, f32[4]{0:T(128)S(1)} %convolution_bitcast_fusion.1), channel_id=1, replica_groups=mesh['dp'=4,'fsdp'=4,'tp'=2] {'fsdp'}, use_global_device_ids=true, to_apply=%region_0.0 | all-reduce | flops 8 | bytes 64 | tf_op jit(solution)/shard_map/psum | solution.py:23
  23.0 5.6 %all-reduce.1 = (f32[4]{0:T(128)S(1)}, f32[4]{0:T(128)S(1)}) all-reduce(f32[4]{0:T(128)S(1)} %get-tuple-element.4, f32[4]{0:T(128)S(1)} %get-tuple-element.5), channel_id=1, replica_groups=mesh['dp'=4,'fsdp'=4,'tp'=2] {'dp'}, use_global_device_ids=true, to_apply=%region_1.0 | all-reduce | flops 8 | bytes 64 | tf_op jit(solution)/shard_map/psum | solution.py:22
  28.7 0.8 convolution_bitcast_fusion.2
  29.5 0.9 fusion.3
  30.4 0.7 divide_bitcast_fusion
  31.1 5.5 %fusion.4 = f32[288,7168]{1,0:T(8,128)S(1)} fusion(bf16[512,7168]{1,0:T(8,128)(2,1)} %param.6, bf16[512,288]{0,1:T(8,128)(2,1)} %param.7, f32[512]{0:T(512)S(1)} %divide_bitcast_fusion), kind=kOutput, calls=%fused_computation.13 | convolution fusion | flops 2114371584 | bytes 15894528 | tf_op jit(solution)/shard_map/td,tc->dc/dot_general | solution.py:43
  36.7 3.8 %copy.18 = f32[36,4,8,1792]{3,2,0,1:T(8,128)} copy(f32[36,4,8,1792]{3,2,1,0:T(8,128)S(1)} %bitcast.43) | data formatting | bytes 16515072 | tf_op jit(solution)/shard_map/reshape | solution.py:45
  40.5 0.0 reduce-scatter.5.cloned.1.call-update
  40.5 0.0 copy-start.1
  40.5 0.0 reduce-scatter.7.cloned.1.call-start
  40.5 141.1 %reduce-scatter.5.cloned.1.call-done = f32[1,1792,288]{1,2,0:T(8,128)} async-done(((f32[4,1792,288]{1,2,0:T(8,128)}), f32[1,1792,288]{1,2,0:T(8,128)}) %reduce-scatter.5.cloned.1.call-update) | async-done | bytes 2064400 | tf_op jit(solution)/shard_map/reduce_scatter | solution.py:44
  181.6 6.9 %copy.12 = f32[1,1792,288]{2,0,1:T(1,128)S(1)} copy(f32[1,1792,288]{1,2,0:T(8,128)} %reduce-scatter.5.cloned.1.call-done) | data formatting | bytes 4128768
  188.5 1.7 copy.19
  190.2 0.0 reduce-scatter.7.cloned.1.call-update
  190.3 0.0 all-gather.2.cloned.1.call-start
  190.3 36.0 %reduce-scatter.7.cloned.1.call-done = f32[448,288]{1,0:T(8,128)} async-done(((f32[1792,288]{1,0:T(8,128)}), f32[448,288]{1,0:T(8,128)}) %reduce-scatter.7.cloned.1.call-update) | async-done | bytes 516112
  226.3 1.6 reshape_bitcast_fusion
  227.9 1.0 copy.13
  228.9 0.0 copy-done.1
  228.9 0.0 copy-start
  228.9 0.1 subtract_convert_fusion
  229.1 9.2 %all_gather.6 = bf16[1,448,576]{1,2,0:T(8,128)(2,1)S(1)} all-gather(bf16[1,448,288]{1,2,0:T(8,128)(2,1)S(1)} %subtract_convert_fusion), channel_id=1, replica_groups=mesh['dp'=4,'fsdp'=4,'tp'=2] {'tp'}, dimensions={2}, use_global_device_ids=true | all-gather | bytes 774144 | tf_op jit(solution)/shard_map/all_gather | solution.py:52
  238.3 1.1 copy.10
  239.4 0.0 all-gather.2.cloned.1.call-update
  239.4 23.8 %all-gather.2.cloned.1.call-done = bf16[1,1792,576]{2,1,0:T(8,128)(2,1)} async-done(((bf16[1,448,576]{2,1,0:T(8,128)(2,1)}), bf16[1,1792,576]{2,1,0:T(8,128)(2,1)}) %all-gather.2.cloned.1.call-update) | async-done | bytes 2064400 | tf_op jit(solution)/shard_map/all_gather | solution.py:53
  263.2 4.1 %copy.11 = bf16[1,1792,576]{1,2,0:T(8,128)(2,1)} copy(bf16[1,1792,576]{2,1,0:T(8,128)(2,1)} %all-gather.2.cloned.1.call-done) | data formatting | bytes 4128768
  267.4 0.0 copy-done
Async XLA Ops:
  7.2 174.5 %reduce-scatter.5.cloned.1.call-start = ((), (), s32[]{:S(2)}) async-start(), calls=%async_computation.2 | async-start | bytes 10321920 | tf_op jit(solution)/shard_map/reduce_scatter | solution.py:44
  40.5 188.4 %copy-start.1 = (f32[1,448,288]{1,2,0:T(8,128)S(1)}, f32[1,448,288]{1,2,0:T(8,128)}, u32[]{:S(2)}) copy-start(f32[1,448,288]{1,2,0:T(8,128)} %param.11) | copy-start | bytes 1548292
  40.5 185.8 %reduce-scatter.7.cloned.1.call-start = ((), (), s32[]{:S(2)}) async-start(), calls=%async_computation.4 | async-start | bytes 3440640
  190.3 73.0 %all-gather.2.cloned.1.call-start = ((), (), s32[]{:S(2)}) async-start(), calls=%async_computation.3 | async-start | bytes 2867200 | tf_op jit(solution)/shard_map/all_gather | solution.py:53
  228.9 38.4 %copy-start = (f32[1,448,288]{1,2,0:T(8,128)}, f32[1,448,288]{1,2,0:T(8,128)S(1)}, u32[]{:S(2)}) copy-start(f32[1,448,288]{1,2,0:T(8,128)S(1)} %copy.13) | copy-start | bytes 1548292
Sparse Core Ops, SparseCore 0:
  40.6 140.9 reduce-scatter.4
  190.4 35.8 reduce-scatter.6
  239.5 23.6 all-gather.1
